TPU v7x, 512 devices: a 4x2x32 block of a 4x8x32 slice. The times are simulated.
512 devices in a mesh: group: 2 (over y), expert: 64 (over z, core), tensor: 4 (over x).
Axes of the slice: x: 4, y: 2, z: 32, core: 2. Of those that a mesh axis runs over, the one named last changes fastest.
The devices are a block of a 4x8x32 slice.
Arguments:
- tokens: bfloat16 [4096, 4096], P(('group', 'expert'), 'tensor'), parts along dimension 0, may hold values from -6 to 6
- expert_ids: int32 [4096, 8], P(('group', 'expert')), parts along dimension 0, may hold values from 0 to 63, all different within a row; in each aligned block of 32 rows (0 to 31, 32 to 63, ...) at most 6 rows name the same one
- router_logits: float32 [4096, 8], P(('group', 'expert')), parts along dimension 0, may hold values from -6 to 6
- up_weight: bfloat16 [64, 4096, 1024], P('expert', None, 'tensor'), may hold values from -0.09375 to 0.09375
- down_weight: bfloat16 [64, 1024, 4096], P('expert', 'tensor'), may hold values from -0.1875 to 0.1875
Outputs:
- moe_out: bfloat16 [4096, 4096], P(('group', 'expert'), 'tensor'), parts along dimension 0
There are 2 independent parts, one for each index of `group`. A program takes and returns all parts, laid end to end along the dimension named above; an argument that names none is the same for every part. Nothing has to cross between parts.
Inputs may be any that keep to these rules, and one draw needn't show every extreme that they name: `expert_ids`: each row names 8 different experts. In each aligned block of 32 rows (the rows of one index of the expert axis) no expert is named by more than 6 rows, a bound that some block reaches.
All inputs are finite; a program needn't handle non-finite values.
Results may differ from a plain program's by a relative error of at most 0.014.
Values may be sent and summed in bfloat16 or wider, within the bound.
No kernel may reach another device: no remote copies, remote signals or barrier semaphores. Data moves between devices by JAX's collectives and lax.ppermute only.
A program may use at most 64 MiB of HBM per device.

v0:
```python
import jax
import jax.numpy as jnp
from jax import lax
from jax.sharding import Mesh
from jax.sharding import PartitionSpec as P

EXPERT = ("expert_0", "expert_1")
GROUP_EXPERT = ("group", "expert_0", "expert_1")


def in_blocks(shard, dim, count):
    shape = shard.shape
    pieces = shard.reshape(*shape[:dim], count, shape[dim] // count, *shape[dim + 1 :])
    return jnp.moveaxis(pieces, dim, 0)


def joined_along(pieces, dim):
    shape = list(pieces.shape[1:])
    shape[dim] *= pieces.shape[0]
    return jnp.moveaxis(pieces, 0, dim).reshape(shape)


def exchange_in_order(pieces, axes, order):
    shape = [lax.axis_size(a) for a in axes]
    pieces = pieces.reshape(*shape, *pieces.shape[1:])
    for k in order:
        pieces = lax.all_to_all(pieces, axes[k], split_axis=k, concat_axis=k, tiled=True)
    return pieces.reshape(-1, *pieces.shape[len(axes) :])


def core_and_chips(shard, groups, order, split_dim, concat_dim):
    count = lax.axis_size(groups[0]) * lax.axis_size(groups[1])
    pieces = in_blocks(shard, split_dim, count)
    return joined_along(exchange_in_order(pieces, groups, order), concat_dim)


def summed_on_arrival(shard, axis, dim):
    count = lax.axis_size(axis)
    pieces = lax.all_to_all(in_blocks(shard, dim, count), axis, 0, 0, tiled=True)
    return jnp.sum(pieces.astype(jnp.float32), axis=0)


def on_device(tokens, expert_ids, router_logits, up_weight, down_weight):
    tok_rows = tokens.shape[0]
    quarter_width = tokens.shape[1]
    top_count = expert_ids.shape[1]
    experts = lax.axis_size(EXPERT)
    capacity = max(2, 3 * tok_rows * top_count // (2 * experts))
    hits = (expert_ids[:, :, None] == jnp.arange(experts, dtype=jnp.int32)[None, None, :]).astype(
        jnp.int32
    )
    per_token = jnp.sum(hits, axis=1)
    rank = jnp.cumsum(per_token, axis=0) - per_token
    slot = jnp.sum(hits * rank[:, None, :], axis=2)
    position = expert_ids * capacity + slot
    placing = position[:, :, None] == jnp.arange(experts * capacity, dtype=jnp.int32)[None, None, :]
    selector = jnp.sum(placing.astype(jnp.float32), axis=1).astype(jnp.bfloat16)
    filled = jnp.einsum("tr,td->rd", selector, tokens, preferred_element_type=jnp.float32)
    outgoing = filled.astype(jnp.bfloat16).reshape(experts, capacity, tokens.shape[1])
    full_rows = lax.all_gather(
        core_and_chips(outgoing, ("expert_0", "expert_1"), (1, 0), 0, 0),
        "tensor",
        axis=2,
        tiled=True,
    )
    width = full_rows.shape[2]
    flat = full_rows.reshape(-1, width)
    act = jnp.dot(flat, up_weight[0], preferred_element_type=jnp.float32)
    hidden = jax.nn.silu(act).astype(jnp.bfloat16)
    part = jnp.dot(hidden, down_weight[0], preferred_element_type=jnp.float32)
    partial_value = part.reshape(full_rows.shape[0], full_rows.shape[1], width)
    shares = summed_on_arrival(partial_value.astype(jnp.bfloat16), "tensor", 2).astype(jnp.bfloat16)
    returned = core_and_chips(shares, ("expert_0", "expert_1"), (1, 0), 0, 0)
    flat_rows = returned.reshape(experts * capacity, quarter_width)
    picked = jnp.take(flat_rows, position.reshape(-1), axis=0).reshape(
        tok_rows, top_count, quarter_width
    )
    gates = jax.nn.sigmoid(router_logits)
    weight = 2.5 * gates / jnp.sum(gates, axis=1, keepdims=True)
    mixed = jnp.sum(weight[:, :, None] * picked.astype(jnp.float32), axis=1)
    return mixed.astype(jnp.bfloat16)


def solution(mesh):
    split = Mesh(
        mesh.devices.reshape(mesh.shape["group"], 32, 2, mesh.shape["tensor"]),
        ("group", "expert_0", "expert_1", "tensor"),
    )
    return jax.shard_map(
        on_device,
        mesh=split,
        in_specs=(
            P(GROUP_EXPERT, "tensor"),
            P(GROUP_EXPERT, None),
            P(GROUP_EXPERT, None),
            P(EXPERT, None, "tensor"),
            P(EXPERT, "tensor", None),
        ),
        out_specs=P(GROUP_EXPERT, "tensor"),
        check_vma=False,
    )
```

profile of v0, /device:TPU:33, one launch (start us, length us, event | category | flops | bytes accessed | tf_op | source)
XLA Modules:
  0.0 381.4 jit_solution(5077829200390835637)
XLA Ops:
  6.5 0.0 copy-start
  6.6 0.0 all-gather.2.cloned.1.call-start
  6.6 0.9 copy.46
  7.5 0.1 convert_reduce_fusion.1
  7.6 0.1 reduce_window_sum.11
  7.6 0.7 select_reduce_fusion
  8.4 0.2 convert_reduce_fusion
  8.5 2.1 convolution_convert_fusion.1
  10.7 1.3 reshape_reshape_reshape.6
  12.0 0.4 copy.48
  12.4 45.4 %all_to_all.25 = bf16[32,2,1,6,1024]{4,0,3,2,1:T(8,128)(2,1)S(1)} all-to-all(bf16[32,2,1,6,1024]{4,0,3,2,1:T(8,128)(2,1)S(1)} %copy.48), channel_id=1, replica_groups=mesh['group'=2,'expert_0'=32,'expert_1'=2,'tensor'=4] {'expert_1'}, dimensions={1} | all-to-all | bytes 1572864 | tf_op jit(solution)/shard_map/all_to_all | solution.py:27
  57.9 0.8 copy.49
  58.7 91.0 %all_to_all.26 = bf16[32,2,1,6,1024]{4,1,3,2,0:T(2,128)(2,1)S(1)} all-to-all(bf16[32,2,1,6,1024]{4,1,3,2,0:T(2,128)(2,1)S(1)} %copy.49), channel_id=1, replica_groups=mesh['group'=2,'expert_0'=32,'expert_1'=2,'tensor'=4] {'expert_0'}, dimensions={0} | all-to-all | bytes 1572864 | tf_op jit(solution)/shard_map/all_to_all | solution.py:27
  149.7 0.5 copy.50
  150.3 1.2 reshape_reshape.6
  151.4 0.1 all-gather.2.cloned.1.call-update
  151.5 39.2 %all-gather.2.cloned.1.call-done = bf16[64,6,4096]{2,0,1:T(8,128)(2,1)} async-done(((bf16[64,6,1024]{2,0,1:T(8,128)(2,1)}), bf16[64,6,4096]{2,0,1:T(8,128)(2,1)}) %all-gather.2.cloned.1.call-update) | async-done | bytes 3145744 | tf_op jit(solution)/shard_map/all_gather | solution.py:60
  190.7 5.6 %copy.51 = bf16[64,6,4096]{2,1,0:T(8,128)(2,1)} copy(bf16[64,6,4096]{2,0,1:T(8,128)(2,1)} %all-gather.2.cloned.1.call-done) | data formatting | bytes 6291456 | tf_op jit(solution)/shard_map/all_gather | solution.py:60
  196.3 5.7 %reshape.64 = bf16[384,4096]{1,0:T(8,128)(2,1)} reshape(bf16[64,6,4096]{2,1,0:T(8,128)(2,1)} %copy.51) | data formatting | bytes 6291456 | tf_op jit(solution)/shard_map/reshape | solution.py:67
  202.0 3.5 multiply_convert_fusion
  205.6 0.1 dot_general.13
  205.7 0.0 copy-done
  205.7 1.0 convolution_convert_fusion
  206.7 0.4 copy.63
  207.1 40.0 %all_to_all.27 = bf16[4,64,6,1024]{3,1,2,0:T(8,128)(2,1)} all-to-all(bf16[4,64,6,1024]{3,1,2,0:T(8,128)(2,1)S(1)} %bitcast.30), channel_id=1, replica_groups=mesh['group'=2,'expert_0'=32,'expert_1'=2,'tensor'=4] {'tensor'}, dimensions={0} | all-to-all | bytes 6291456 | tf_op jit(solution)/shard_map/all_to_all | solution.py:39
  247.1 3.6 reduce_sum.61
  250.7 2.1 reshape_reshape.7
  252.8 0.0 copy-start.1
  252.9 0.2 copy.55
  253.1 6.0 %all_to_all.28 = bf16[32,2,1,6,1024]{4,0,3,2,1:T(8,128)(2,1)S(1)} all-to-all(bf16[32,2,1,6,1024]{4,0,3,2,1:T(8,128)(2,1)S(1)} %copy.55), channel_id=1, replica_groups=mesh['group'=2,'expert_0'=32,'expert_1'=2,'tensor'=4] {'expert_1'}, dimensions={1} | all-to-all | bytes 1572864 | tf_op jit(solution)/shard_map/all_to_all | solution.py:27
  259.1 1.7 copy.56
  260.7 23.2 %all-to-all-start.4 = ((bf16[32,2,1,6,1024]{4,1,3,2,0:T(2,128)(2,1)}), bf16[32,2,1,6,1024]{4,1,3,2,0:T(2,128)(2,1)S(1)}, u32[]{:S(2)}, u32[]{:S(2)}) async-start(bf16[32,2,1,6,1024]{4,1,3,2,0:T(2,128)(2,1)} %copy.56), calls=%async_computation.4 | async-start | bytes 1572864 | tf_op jit(solution)/shard_map/all_to_all | solution.py:27
  283.9 0.1 reshape.66
  284.0 0.0 copy-done.1
  284.1 0.1 copy.45
  284.2 85.5 %all-to-all-done.4 = bf16[32,2,1,6,1024]{4,1,3,2,0:T(2,128)(2,1)S(1)} async-done(((bf16[32,2,1,6,1024]{4,1,3,2,0:T(2,128)(2,1)}), bf16[32,2,1,6,1024]{4,1,3,2,0:T(2,128)(2,1)S(1)}, u32[]{:S(2)}, u32[]{:S(2)}) %all-to-all-start.4) | async-done | bytes 786464 | tf_op jit(solution)/shard_map/all_to_all | solution.py:27
  369.6 1.2 copy.57
  370.9 1.4 reshape_reshape_reshape.7
  372.3 1.2 gather_fusion
  373.5 1.1 multiply_reduce_fusion
  (6 shorter events, 0.1 us)
Async XLA Ops:
  6.5 199.1 %copy-start = (bf16[1,256,4096]{2,1,0:T(8,128)(2,1)S(1)}, bf16[1,256,4096]{2,1,0:T(8,128)(2,1)}, u32[]{:S(2)}) copy-start(bf16[1,256,4096]{2,1,0:T(8,128)(2,1)} %param.9) | copy-start | bytes 6291460
  6.6 184.2 %all-gather.2.cloned.1.call-start = ((), (), s32[]{:S(2)}) async-start(), calls=%async_computation.5 | async-start | bytes 3932160 | tf_op jit(solution)/shard_map/all_gather | solution.py:60
  252.8 31.2 %copy-start.1 = (f32[32,8]{0,1:T(8,128)S(1)}, f32[32,8]{0,1:T(8,128)}, u32[]{:S(2)}) copy-start(f32[32,8]{0,1:T(8,128)} %param.7) | copy-start | bytes 3076
  260.7 108.9 %all-to-all-start.4 = ((bf16[32,2,1,6,1024]{4,1,3,2,0:T(2,128)(2,1)}), bf16[32,2,1,6,1024]{4,1,3,2,0:T(2,128)(2,1)S(1)}, u32[]{:S(2)}, u32[]{:S(2)}) async-start(bf16[32,2,1,6,1024]{4,1,3,2,0:T(2,128)(2,1)} %copy.56), calls=%async_computation.4 | async-start | bytes 1572864 | tf_op jit(solution)/shard_map/all_to_all | solution.py:27
Sparse Core Ops, SparseCore 0:
  151.6 39.0 all-gather.1
where the time goes:
time: 382 us; the launch traced here: 381 us
  blocking collectives  182 us (48%)
  waiting for transfers between devices  125 us (33%)
  local copies, waits for them, and re-layouts  25 us (7%)
  starting transfers between devices  23.2 us (6%)
  between operations  13.6 us (4%)
  matrix products  6.63 us (2%)
  other arithmetic  5.84 us (2%)
    all_to_all x3, blocking collectives, exchange_in_order(): lax.all_to_all(pieces, axes[k], split_axis=k, concat_axis=k, tiled=True)  142 us
    all_to_all x1, waiting for transfers between devices, exchange_in_order(): lax.all_to_all(pieces, axes[k], split_axis=k, concat_axis=k, tiled=True)  85.5 us
    all_to_all x1, blocking collectives, summed_on_arrival(): lax.all_to_all(in_blocks(shard, dim, count), axis, 0, 0, tiled=True)  40 us
    all_gather x1, waiting for transfers between devices, on_device(): lax.all_gather(core_and_chips(outgoing, ('expert_0', 'expert_1'), (1, 0),...  39.2 us
    all_to_all x1, starting transfers between devices, exchange_in_order(): lax.all_to_all(pieces, axes[k], split_axis=k, concat_axis=k, tiled=True)  23.2 us
  transfers between devices with their start and end apart: 2, of which 2 were waited for; matrix products, arithmetic and copies ran while one was open for 0% of the time, Pallas kernels for 0%

commit v1 on v0

--- a/solution.py
+++ b/solution.py
@@ -57,12 +57,25 @@
     selector = jnp.sum(placing.astype(jnp.float32), axis=1).astype(jnp.bfloat16)
     filled = jnp.einsum("tr,td->rd", selector, tokens, preferred_element_type=jnp.float32)
     outgoing = filled.astype(jnp.bfloat16).reshape(experts, capacity, tokens.shape[1])
-    full_rows = lax.all_gather(
-        core_and_chips(outgoing, ("expert_0", "expert_1"), (1, 0), 0, 0),
-        "tensor",
-        axis=2,
-        tiled=True,
+    array = core_and_chips(outgoing, ("expert_0", "expert_1"), (1, 0), 0, 0)
+    ways, here, step = (lax.axis_size("tensor"), lax.axis_index("tensor"), array.shape[2])
+    dims = [n * ways if d == 2 else n for d, n in enumerate(array.shape)]
+    full_rows = lax.dynamic_update_slice_in_dim(
+        jnp.zeros(dims, array.dtype), array, here * step, axis=2
     )
+    going_up = going_down = array
+    for far in range(1, ways // 2 + 1):
+        going_up = lax.ppermute(going_up, "tensor", [(d, (d + 1) % ways) for d in range(ways)])
+        full_rows = lax.dynamic_update_slice_in_dim(
+            full_rows, going_up, (here - far) % ways * step, axis=2
+        )
+        if 2 * far < ways:
+            going_down = lax.ppermute(
+                going_down, "tensor", [(d, (d - 1) % ways) for d in range(ways)]
+            )
+            full_rows = lax.dynamic_update_slice_in_dim(
+                full_rows, going_down, (here + far) % ways * step, axis=2
+            )
     width = full_rows.shape[2]
     flat = full_rows.reshape(-1, width)
     act = jnp.dot(flat, up_weight[0], preferred_element_type=jnp.float32)

time: 382 us -> 352 us (0.921)
  waiting for transfers between devices: 125 us -> 109 us
  between operations: 13.6 us -> 0.24 us
  starting transfers between devices: 23.2 us -> 15.4 us
  local copies, waits for them, and re-layouts: 25 us -> 32 us
    all_gather x1 -> x0, waiting for transfers between devices: 39.2 us -> none  [on_device(): lax.all_gather(core_and_chips(outgoing, ('expert_0', 'expert_1'), (1, 0),...]
    ppermute x0 -> x3, waiting for transfers between devices: none -> 23.4 us  [the longest x2 23.4 us: on_device(): lax.ppermute(going_up, 'tensor', [(d, (d + 1) % ways) for d in range(ways)])]
    all_to_all x1, starting transfers between devices: 23.2 us -> 6.66 us  [exchange_in_order(): lax.all_to_all(pieces, axes[k], split_axis=k, concat_axis=k, tiled=True)]
    ppermute x0 -> x3, starting transfers between devices: none -> 8.71 us  [the longest x2 5.22 us: on_device(): lax.ppermute(going_up, 'tensor', [(d, (d + 1) % ways) for d in range(ways)])]
    dynamic_update_slice x0 -> x4, local copies, waits for them, and re-layouts: none -> 8.19 us  [the longest x2 4.04 us: on_device(): lax.dynamic_update_slice_in_dim(full_rows, going_up, (here - far) % ways...]
    all_gather x1 -> x0, local copies, waits for them, and re-layouts: 5.57 us -> none  [on_device(): lax.all_gather(core_and_chips(outgoing, ('expert_0', 'expert_1'), (1, 0),...]
  transfers between devices with their start and end apart: 2 -> 4, of which waited for: 2 -> 3; matrix products, arithmetic and copies ran while one was open for 0% -> 3% of each run, Pallas kernels for 0% -> 0%
where the time goes in v1:
time: 352 us; the launch traced here: 351 us
  blocking collectives  182 us (52%)
  waiting for transfers between devices  109 us (31%)
  local copies, waits for them, and re-layouts  32 us (9%)
  starting transfers between devices  15.4 us (4%)
  matrix products  6.63 us (2%)
  other arithmetic  5.84 us (2%)
    all_to_all x3, blocking collectives, exchange_in_order(): lax.all_to_all(pieces, axes[k], split_axis=k, concat_axis=k, tiled=True)  144 us
    all_to_all x1, waiting for transfers between devices, exchange_in_order(): lax.all_to_all(pieces, axes[k], split_axis=k, concat_axis=k, tiled=True)  85.5 us
    all_to_all x1, blocking collectives, summed_on_arrival(): lax.all_to_all(in_blocks(shard, dim, count), axis, 0, 0, tiled=True)  37.9 us
    ppermute x2, waiting for transfers between devices, on_device(): lax.ppermute(going_up, 'tensor', [(d, (d + 1) % ways) for d in range(ways)])  23.4 us
  transfers between devices with their start and end apart: 4, of which 3 were waited for; matrix products, arithmetic and copies ran while one was open for 3% of the time, Pallas kernels for 0%

profile of v1, /device:TPU:33, one launch (start us, length us, event | category | flops | bytes accessed | tf_op | source)
XLA Modules:
  0.0 351.4 jit_solution(12217453222511121391)
XLA Ops:
  0.0 0.0 copy-start
  0.0 0.9 copy.53
  0.9 0.1 convert_reduce_fusion.1
  1.0 0.1 reduce_window_sum.11
  1.1 0.7 select_reduce_fusion
  1.8 0.2 convert_reduce_fusion
  2.0 2.1 convolution_convert_fusion.1
  4.1 1.3 reshape_reshape_reshape.6
  5.4 0.4 copy.55
  5.9 45.4 %all_to_all.25 = bf16[32,2,1,6,1024]{4,0,3,2,1:T(8,128)(2,1)S(1)} all-to-all(bf16[32,2,1,6,1024]{4,0,3,2,1:T(8,128)(2,1)S(1)} %copy.55), channel_id=1, replica_groups=mesh['group'=2,'expert_0'=32,'expert_1'=2,'tensor'=4] {'expert_1'}, dimensions={1} | all-to-all | bytes 1572864 | tf_op jit(solution)/shard_map/all_to_all | solution.py:27
  51.3 0.8 copy.56
  52.1 91.0 %all_to_all.26 = bf16[32,2,1,6,1024]{4,1,3,2,0:T(2,128)(2,1)S(1)} all-to-all(bf16[32,2,1,6,1024]{4,1,3,2,0:T(2,128)(2,1)S(1)} %copy.56), channel_id=1, replica_groups=mesh['group'=2,'expert_0'=32,'expert_1'=2,'tensor'=4] {'expert_0'}, dimensions={0} | all-to-all | bytes 1572864 | tf_op jit(solution)/shard_map/all_to_all | solution.py:27
  143.2 1.4 copy.57
  144.6 2.3 reshape_reshape.6
  146.9 3.3 collective-permute-start
  150.1 3.5 collective-permute-start.1
  153.7 14.3 %collective-permute-done = bf16[64,6,1024]{2,0,1:T(8,128)(2,1)} collective-permute-done((bf16[64,6,1024]{2,0,1:T(8,128)(2,1)S(1)}, bf16[64,6,1024]{2,0,1:T(8,128)(2,1)}, u32[]{:S(2)}, u32[]{:S(2)}) %collective-permute-start) | collective-permute-done | bytes 786464 | tf_op jit(solution)/shard_map/ppermute | solution.py:68
  168.0 1.9 collective-permute-start.2
  170.0 2.4 broadcast_in_dim.13
  172.4 1.5 copy_dynamic-update-slice_fusion.3
  173.9 2.6 copy_dynamic-update-slice_fusion.2
  176.5 0.0 collective-permute-done.1
  176.5 2.7 copy_dynamic-update-slice_fusion.1
  179.1 9.1 %collective-permute-done.2 = bf16[64,6,1024]{2,0,1:T(8,128)(2,1)S(1)} collective-permute-done((bf16[64,6,1024]{2,0,1:T(8,128)(2,1)}, bf16[64,6,1024]{2,0,1:T(8,128)(2,1)S(1)}, u32[]{:S(2)}, u32[]{:S(2)}) %collective-permute-start.2) | collective-permute-done | bytes 786464 | tf_op jit(solution)/shard_map/ppermute | solution.py:68
  188.2 1.5 copy_dynamic-update-slice_fusion
  189.7 5.7 %reshape.64 = bf16[384,4096]{1,0:T(8,128)(2,1)} reshape(bf16[64,6,4096]{2,1,0:T(8,128)(2,1)} %copy_dynamic-update-slice_fusion) | data formatting | bytes 6291456 | tf_op jit(solution)/shard_map/reshape | solution.py:80
  195.4 3.5 %multiply_convert_fusion = bf16[384,256]{1,0:T(8,128)(2,1)S(1)} fusion(bf16[384,4096]{1,0:T(8,128)(2,1)} %reshape.64, bf16[1,4096,256]{2,1,0:T(8,128)(2,1)} %param.8), kind=kOutput, calls=%fused_computation.13 | convolution fusion | flops 805797888 | bytes 5439488 | tf_op jit(solution)/shard_map/dot_general | solution.py:81
  199.0 0.1 dot_general.13
  199.0 0.0 copy-done
  199.0 1.0 convolution_convert_fusion
  200.0 0.4 copy.77
  200.5 37.9 %all_to_all.27 = bf16[4,64,6,1024]{3,1,2,0:T(8,128)(2,1)} all-to-all(bf16[4,64,6,1024]{3,1,2,0:T(8,128)(2,1)S(1)} %bitcast.30), channel_id=1, replica_groups=mesh['group'=2,'expert_0'=32,'expert_1'=2,'tensor'=4] {'tensor'}, dimensions={0} | all-to-all | bytes 6291456 | tf_op jit(solution)/shard_map/all_to_all | solution.py:39
  238.4 3.6 %reduce_sum.61 = bf16[64,6,1024]{2,0,1:T(8,128)(2,1)} reduce(bf16[4,64,6,1024]{3,1,2,0:T(8,128)(2,1)} %all_to_all.27, bf16[]{:T(256)} %constant.59.clone.1), dimensions={0}, to_apply=%region_5.6 | reduce | flops 1179648 | bytes 3932162 | tf_op jit(solution)/shard_map/reduce_sum | solution.py:40
  242.0 2.1 reshape_reshape.7
  244.2 0.0 copy-start.1
  244.2 0.2 copy.65
  244.4 8.0 %all_to_all.28 = bf16[32,2,1,6,1024]{4,0,3,2,1:T(8,128)(2,1)S(1)} all-to-all(bf16[32,2,1,6,1024]{4,0,3,2,1:T(8,128)(2,1)S(1)} %copy.65), channel_id=1, replica_groups=mesh['group'=2,'expert_0'=32,'expert_1'=2,'tensor'=4] {'expert_1'}, dimensions={1} | all-to-all | bytes 1572864 | tf_op jit(solution)/shard_map/all_to_all | solution.py:27
  252.4 1.7 copy.66
  254.1 6.7 %all-to-all-start.4 = ((bf16[32,2,1,6,1024]{4,1,3,2,0:T(2,128)(2,1)}), bf16[32,2,1,6,1024]{4,1,3,2,0:T(2,128)(2,1)S(1)}, u32[]{:S(2)}, u32[]{:S(2)}) async-start(bf16[32,2,1,6,1024]{4,1,3,2,0:T(2,128)(2,1)} %copy.66), calls=%async_computation.4 | async-start | bytes 1572864 | tf_op jit(solution)/shard_map/all_to_all | solution.py:27
  260.7 0.1 reshape.66
  260.8 0.0 copy-done.1
  260.9 0.1 copy.52
  261.0 85.5 %all-to-all-done.4 = bf16[32,2,1,6,1024]{4,1,3,2,0:T(2,128)(2,1)S(1)} async-done(((bf16[32,2,1,6,1024]{4,1,3,2,0:T(2,128)(2,1)}), bf16[32,2,1,6,1024]{4,1,3,2,0:T(2,128)(2,1)S(1)}, u32[]{:S(2)}, u32[]{:S(2)}) %all-to-all-start.4) | async-done | bytes 786464 | tf_op jit(solution)/shard_map/all_to_all | solution.py:27
  346.5 1.2 copy.67
  347.7 1.4 reshape_reshape_reshape.7
  349.1 1.2 gather_fusion
  350.3 1.1 multiply_reduce_fusion
  (6 shorter events, 0.1 us)
Async XLA Ops:
  0.0 199.0 %copy-start = (bf16[1,256,4096]{2,1,0:T(8,128)(2,1)S(1)}, bf16[1,256,4096]{2,1,0:T(8,128)(2,1)}, u32[]{:S(2)}) copy-start(bf16[1,256,4096]{2,1,0:T(8,128)(2,1)} %param.9) | copy-start | bytes 6291460
  146.9 21.2 %collective-permute-start = (bf16[64,6,1024]{2,0,1:T(8,128)(2,1)S(1)}, bf16[64,6,1024]{2,0,1:T(8,128)(2,1)}, u32[]{:S(2)}, u32[]{:S(2)}) collective-permute-start(bf16[64,6,1024]{2,0,1:T(8,128)(2,1)S(1)} %reshape_reshape.6), channel_id=1, source_target_pairs={{0,1},{1,2},{2,3},{3,0},{4,5},{5,6},{6,7},{7,4},{8,9},{9,10},{10,1... | collective-permute-start | bytes 2359304 | tf_op jit(solution)/shard_map/ppermute | solution.py:68
  150.1 26.3 %collective-permute-start.1 = (bf16[64,6,1024]{2,0,1:T(8,128)(2,1)S(1)}, bf16[64,6,1024]{2,0,1:T(8,128)(2,1)}, u32[]{:S(2)}, u32[]{:S(2)}) collective-permute-start(bf16[64,6,1024]{2,0,1:T(8,128)(2,1)S(1)} %reshape_reshape.6), channel_id=1, source_target_pairs={{0,3},{1,0},{2,1},{3,2},{4,7},{5,4},{6,5},{7,6},{8,11},{9,8},{10,9... | collective-permute-start | bytes 2359304 | tf_op jit(solution)/shard_map/ppermute | solution.py:73
  168.0 20.2 %collective-permute-start.2 = (bf16[64,6,1024]{2,0,1:T(8,128)(2,1)}, bf16[64,6,1024]{2,0,1:T(8,128)(2,1)S(1)}, u32[]{:S(2)}, u32[]{:S(2)}) collective-permute-start(bf16[64,6,1024]{2,0,1:T(8,128)(2,1)} %collective-permute-done), channel_id=1, source_target_pairs={{0,1},{1,2},{2,3},{3,0},{4,5},{5,6},{6,7},{7,4},{8,9},{9,10},{10,1... | collective-permute-start | bytes 2359304 | tf_op jit(solution)/shard_map/ppermute | solution.py:68
  244.2 16.6 %copy-start.1 = (f32[32,8]{0,1:T(8,128)S(1)}, f32[32,8]{0,1:T(8,128)}, u32[]{:S(2)}) copy-start(f32[32,8]{0,1:T(8,128)} %param.7) | copy-start | bytes 3076
  254.1 92.4 %all-to-all-start.4 = ((bf16[32,2,1,6,1024]{4,1,3,2,0:T(2,128)(2,1)}), bf16[32,2,1,6,1024]{4,1,3,2,0:T(2,128)(2,1)S(1)}, u32[]{:S(2)}, u32[]{:S(2)}) async-start(bf16[32,2,1,6,1024]{4,1,3,2,0:T(2,128)(2,1)} %copy.66), calls=%async_computation.4 | async-start | bytes 1572864 | tf_op jit(solution)/shard_map/all_to_all | solution.py:27
